TPU v7x, 32 devices: a whole 2x2x4 slice. The times are simulated.
32 devices in a mesh: fsdp: 8 (over z, y), seq: 4 (over x, core).
Axes of the slice: x: 2, y: 2, z: 4, core: 2. Of those that a mesh axis runs over, the one named last changes fastest.
Arguments:
- tokens: bfloat16 [8, 1024, 1152], P('fsdp', 'seq'), may hold values from -6 to 6
- condition: float32 [8, 1152], P('fsdp'), may hold values from -6 to 6
- w_ada: bfloat16 [1152, 6912], P('fsdp'), may hold values from -0.1875 to 0.1875
- b_ada: bfloat16 [6912], P('fsdp'), may hold values from -3 to 3
- w_qkv: bfloat16 [1152, 3456], P('fsdp'), may hold values from -0.1875 to 0.1875
- b_qv: bfloat16 [2, 1152], P(None, 'fsdp'), may hold values from -3 to 3
- w_out: bfloat16 [1152, 1152], P('fsdp'), may hold values from -0.75 to 0.75
- b_out: bfloat16 [1152], P('fsdp'), may hold values from -3 to 3
- w_up: bfloat16 [1152, 4608], P('fsdp'), may hold values from -0.1875 to 0.1875
- b_up: bfloat16 [4608], P('fsdp'), may hold values from -3 to 3
- w_down: bfloat16 [4608, 1152], P('fsdp'), may hold values from -0.09375 to 0.09375
- b_down: bfloat16 [1152], P('fsdp'), may hold values from -3 to 3
- grad_output: bfloat16 [8, 1024, 1152], P('fsdp', 'seq'), may hold values from -6 to 6
Outputs:
- output: bfloat16 [8, 1024, 1152], P('fsdp', 'seq')
- grad_tokens: bfloat16 [8, 1024, 1152], P('fsdp', 'seq')
- grad_condition: float32 [8, 1152], P('fsdp')
- grad_w_ada: float32 [1152, 6912], P('fsdp')
- grad_b_ada: float32 [6912], P('fsdp')
- grad_w_qkv: float32 [1152, 3456], P('fsdp')
- grad_b_qv: float32 [2, 1152], P(None, 'fsdp')
- grad_w_out: float32 [1152, 1152], P('fsdp')
- grad_b_out: float32 [1152], P('fsdp')
- grad_w_up: float32 [1152, 4608], P('fsdp')
- grad_b_up: float32 [4608], P('fsdp')
- grad_w_down: float32 [4608, 1152], P('fsdp')
- grad_b_down: float32 [1152], P('fsdp')
All inputs are finite; a program needn't handle non-finite values.
Results may differ from a plain program's by a relative error of at most 0.018.
Values may be sent and summed in bfloat16 or wider, within the bound.
A program may use at most 320 MiB of HBM per device.

v0:
```python
import jax
import jax.numpy as jnp
from jax import lax
from jax.sharding import PartitionSpec as P

HD = 72
EPSILON = 1e-06
GELU_C = 0.7978845608028654


def layer_norm(values):
    mean_val = jnp.mean(values, axis=-1, keepdims=True)
    centred = values - mean_val
    inv_std = lax.rsqrt(jnp.mean(centred * centred, axis=-1, keepdims=True) + EPSILON)
    return (centred * inv_std, inv_std)


def norm_back(grad_norm, normed, inv_std):
    first = jnp.mean(grad_norm, axis=-1, keepdims=True)
    second = jnp.mean(grad_norm * normed, axis=-1, keepdims=True)
    return inv_std * (grad_norm - first - normed * second)


def gelu_tanh(values):
    inner = GELU_C * (values + 0.044715 * values * values * values)
    return 0.5 * values * (1.0 + jnp.tanh(inner))


def gelu_slope(values):
    inner = GELU_C * (values + 0.044715 * values * values * values)
    tanh_val = jnp.tanh(inner)
    return 0.5 * (1.0 + tanh_val) + 0.5 * values * (1.0 - tanh_val * tanh_val) * GELU_C * (
        1.0 + 3.0 * 0.044715 * values * values
    )


def matmul(left, right):
    return jnp.dot(left, right, preferred_element_type=jnp.float32)


def matmul_tn(left, right):
    return lax.dot_general(
        left, right, (((0,), (0,)), ((), ())), preferred_element_type=jnp.float32
    )


def matmul_nt(left, right):
    return lax.dot_general(
        left, right, (((1,), (1,)), ((), ())), preferred_element_type=jnp.float32
    )


def head_scores(query, key):
    factor = HD ** (-0.5)
    return jnp.einsum("qhd,khd->hqk", query, key, preferred_element_type=jnp.float32) * factor


def attend_latent(items):
    query, key, value = items
    seq_full = query.shape[0]
    heads_here = query.shape[1] // HD
    query = query.reshape(seq_full, heads_here, HD)
    key = key.reshape(seq_full, heads_here, HD)
    value = value.reshape(seq_full, heads_here, HD)
    scores = head_scores(query, key)
    highest = jnp.max(scores, axis=-1, keepdims=True)
    log_total = highest + jnp.log(jnp.sum(jnp.exp(scores - highest), axis=-1, keepdims=True))
    probs = jnp.exp(scores - log_total).astype(jnp.bfloat16)
    mixed = jnp.einsum("hqk,khd->qhd", probs, value, preferred_element_type=jnp.float32)
    return (mixed.astype(jnp.bfloat16).reshape(seq_full, heads_here * HD), log_total)


def attend_latent_back(items):
    query, key, value, mixed, log_total, grad_mix = items
    factor = HD ** (-0.5)
    seq_full = query.shape[0]
    heads_here = query.shape[1] // HD
    shape_heads = (seq_full, heads_here, HD)
    query = query.reshape(shape_heads)
    key = key.reshape(shape_heads)
    value = value.reshape(shape_heads)
    mixed = mixed.reshape(shape_heads)
    grad_mix = grad_mix.reshape(shape_heads)
    probs = jnp.exp(head_scores(query, key) - log_total)
    delta = jnp.sum(grad_mix.astype(jnp.float32) * mixed.astype(jnp.float32), axis=-1)
    grad_probs = jnp.einsum("qhd,khd->hqk", grad_mix, value, preferred_element_type=jnp.float32)
    grad_scores = (probs * (grad_probs - jnp.transpose(delta)[:, :, None]) * factor).astype(
        jnp.bfloat16
    )
    grad_query = jnp.einsum("hqk,khd->qhd", grad_scores, key, preferred_element_type=jnp.float32)
    grad_key = jnp.einsum("hqk,qhd->khd", grad_scores, query, preferred_element_type=jnp.float32)
    grad_value = jnp.einsum(
        "hqk,qhd->khd", probs.astype(jnp.bfloat16), grad_mix, preferred_element_type=jnp.float32
    )
    flat = (seq_full, heads_here * HD)
    return (
        grad_query.astype(jnp.bfloat16).reshape(flat),
        grad_key.astype(jnp.bfloat16).reshape(flat),
        grad_value.astype(jnp.bfloat16).reshape(flat),
    )


def token_sums(values):
    return jnp.sum(values, axis=1)


def local(
    tokens,
    condition,
    w_ada,
    b_ada,
    w_qkv,
    b_qv,
    w_out,
    b_out,
    w_up,
    b_up,
    w_down,
    b_down,
    grad_output,
):
    lat_dev, seq_loc, width = tokens.shape
    row_count = lat_dev * seq_loc
    full_qkv, full_bqv, full_out, full_bout, full_up, full_bup, full_down, full_bdown, full_bada = (
        lax.all_gather(w_qkv, "fsdp", axis=0, tiled=True),
        lax.all_gather(b_qv, "fsdp", axis=1, tiled=True),
        lax.all_gather(w_out, "fsdp", axis=0, tiled=True),
        lax.all_gather(b_out, "fsdp", axis=0, tiled=True),
        lax.all_gather(w_up, "fsdp", axis=0, tiled=True),
        lax.all_gather(b_up, "fsdp", axis=0, tiled=True),
        lax.all_gather(w_down, "fsdp", axis=0, tiled=True),
        lax.all_gather(b_down, "fsdp", axis=0, tiled=True),
        lax.all_gather(b_ada, "fsdp", axis=0, tiled=True),
    )
    attn_width = full_out.shape[0]
    cond_sig = jax.nn.sigmoid(condition)
    cond_act = (condition * cond_sig).astype(jnp.bfloat16)
    full_ada = lax.all_gather(w_ada, "fsdp", axis=0, tiled=True)
    mods = matmul(cond_act, full_ada) + full_bada.astype(jnp.float32)
    mods = mods.reshape(lat_dev, 6, 1, width)
    shift_attn, scale_attn, gate_attn = (mods[:, 0], mods[:, 1], mods[:, 2])
    shift_ff, scale_ff, gate_ff = (mods[:, 3], mods[:, 4], mods[:, 5])
    source = tokens.astype(jnp.float32)
    normed1, inv1 = layer_norm(source)
    hidden1 = (
        (normed1 * (1.0 + scale_attn) + shift_attn).astype(jnp.bfloat16).reshape(row_count, width)
    )
    qkv = matmul(hidden1, full_qkv)
    tok_shape = (lat_dev, seq_loc, attn_width)
    query = (
        (qkv[:, :attn_width] + full_bqv[0].astype(jnp.float32))
        .astype(jnp.bfloat16)
        .reshape(tok_shape)
    )
    key = qkv[:, attn_width : 2 * attn_width].astype(jnp.bfloat16).reshape(tok_shape)
    value = (
        (qkv[:, 2 * attn_width :] + full_bqv[1].astype(jnp.float32))
        .astype(jnp.bfloat16)
        .reshape(tok_shape)
    )
    heads_q, heads_k, heads_v = (
        lax.all_to_all(query, "seq", split_axis=2, concat_axis=1, tiled=True),
        lax.all_to_all(key, "seq", split_axis=2, concat_axis=1, tiled=True),
        lax.all_to_all(value, "seq", split_axis=2, concat_axis=1, tiled=True),
    )
    mixed_heads, log_totals = lax.map(attend_latent, (heads_q, heads_k, heads_v))
    attn_mix = lax.all_to_all(mixed_heads, "seq", split_axis=1, concat_axis=2, tiled=True).reshape(
        row_count, attn_width
    )
    attn_out = (matmul(attn_mix, full_out) + full_bout.astype(jnp.float32)).reshape(
        lat_dev, seq_loc, width
    )
    resid1 = source + gate_attn * attn_out
    normed2, inv2 = layer_norm(resid1)
    hidden2 = (normed2 * (1.0 + scale_ff) + shift_ff).astype(jnp.bfloat16).reshape(row_count, width)
    pre_act = matmul(hidden2, full_up) + full_bup.astype(jnp.float32)
    activated = gelu_tanh(pre_act).astype(jnp.bfloat16)
    ff_out = (matmul(activated, full_down) + full_bdown.astype(jnp.float32)).reshape(
        lat_dev, seq_loc, width
    )
    output = (resid1 + gate_ff * ff_out).astype(jnp.bfloat16)
    back_qkv, back_out, back_up, back_down = (
        lax.all_gather(w_qkv, "fsdp", axis=0, tiled=True),
        lax.all_gather(w_out, "fsdp", axis=0, tiled=True),
        lax.all_gather(w_up, "fsdp", axis=0, tiled=True),
        lax.all_gather(w_down, "fsdp", axis=0, tiled=True),
    )
    grad_y = grad_output.astype(jnp.float32)
    grad_ff = (grad_y * gate_ff).reshape(row_count, width)
    grad_ff_low = grad_ff.astype(jnp.bfloat16)
    grad_w_down = matmul_tn(activated, grad_ff_low)
    grad_b_down = jnp.sum(grad_ff, axis=0)
    grad_pre = matmul_nt(grad_ff_low, back_down) * gelu_slope(pre_act)
    grad_pre_low = grad_pre.astype(jnp.bfloat16)
    grad_w_up = matmul_tn(hidden2, grad_pre_low)
    grad_b_up = jnp.sum(grad_pre, axis=0)
    grad_h2 = matmul_nt(grad_pre_low, back_up).reshape(lat_dev, seq_loc, width)
    grad_resid1 = grad_y + norm_back(grad_h2 * (1.0 + scale_ff), normed2, inv2)
    grad_attn = (grad_resid1 * gate_attn).reshape(row_count, width)
    grad_attn_low = grad_attn.astype(jnp.bfloat16)
    grad_w_out = matmul_tn(attn_mix, grad_attn_low)
    grad_b_out = jnp.sum(grad_attn, axis=0)
    grad_mix = matmul_nt(grad_attn_low, back_out).astype(jnp.bfloat16).reshape(tok_shape)
    grad_mix_heads = lax.all_to_all(grad_mix, "seq", split_axis=2, concat_axis=1, tiled=True)
    grad_qh, grad_kh, grad_vh = lax.map(
        attend_latent_back, (heads_q, heads_k, heads_v, mixed_heads, log_totals, grad_mix_heads)
    )
    grad_q, grad_k, grad_v = (
        lax.all_to_all(grad_qh, "seq", split_axis=1, concat_axis=2, tiled=True),
        lax.all_to_all(grad_kh, "seq", split_axis=1, concat_axis=2, tiled=True),
        lax.all_to_all(grad_vh, "seq", split_axis=1, concat_axis=2, tiled=True),
    )
    grad_qkv = jnp.concatenate([grad_q, grad_k, grad_v], axis=2).reshape(row_count, 3 * attn_width)
    grad_w_qkv = matmul_tn(hidden1, grad_qkv)
    grad_b_qv = jnp.stack(
        [
            jnp.sum(grad_q.astype(jnp.float32), axis=(0, 1)),
            jnp.sum(grad_v.astype(jnp.float32), axis=(0, 1)),
        ]
    )
    grad_h1 = matmul_nt(grad_qkv, back_qkv).reshape(lat_dev, seq_loc, width)
    grad_tokens = (grad_resid1 + norm_back(grad_h1 * (1.0 + scale_attn), normed1, inv1)).astype(
        jnp.bfloat16
    )
    grad_mods = jnp.stack(
        [
            token_sums(grad_h1),
            token_sums(grad_h1 * normed1),
            token_sums(grad_resid1 * attn_out),
            token_sums(grad_h2),
            token_sums(grad_h2 * normed2),
            token_sums(grad_y * ff_out),
        ],
        axis=1,
    )
    grad_mods_low = grad_mods.reshape(lat_dev, 6 * width).astype(jnp.bfloat16)
    grad_b_ada = jnp.sum(grad_mods_low.astype(jnp.float32), axis=0)
    grad_w_ada = lax.psum_scatter(
        matmul_tn(cond_act, grad_mods_low).astype(jnp.bfloat16),
        "fsdp",
        scatter_dimension=0,
        tiled=True,
    )
    grad_cond_act = matmul_nt(grad_mods_low, full_ada)
    grad_cond_part = grad_cond_act * cond_sig * (1.0 + condition * (1.0 - cond_sig))
    s_wqkv, s_bqv, s_wout, s_bout, s_wup, s_bup, s_wdown, s_bdown, s_bada = (
        lax.psum_scatter(grad_w_qkv, ("fsdp", "seq"), scatter_dimension=0, tiled=True),
        lax.psum_scatter(grad_b_qv, ("fsdp", "seq"), scatter_dimension=1, tiled=True),
        lax.psum_scatter(grad_w_out, ("fsdp", "seq"), scatter_dimension=0, tiled=True),
        lax.psum_scatter(grad_b_out, ("fsdp", "seq"), scatter_dimension=0, tiled=True),
        lax.psum_scatter(grad_w_up, ("fsdp", "seq"), scatter_dimension=0, tiled=True),
        lax.psum_scatter(grad_b_up, ("fsdp", "seq"), scatter_dimension=0, tiled=True),
        lax.psum_scatter(grad_w_down, ("fsdp", "seq"), scatter_dimension=0, tiled=True),
        lax.psum_scatter(grad_b_down, ("fsdp", "seq"), scatter_dimension=0, tiled=True),
        lax.psum_scatter(grad_b_ada, ("fsdp", "seq"), scatter_dimension=0, tiled=True),
    )
    t_wqkv, t_bqv, t_wout, t_bout, t_wup, t_bup, t_wdown, t_bdown, t_bada = (
        lax.all_gather(s_wqkv.astype(jnp.bfloat16), "seq", axis=0, tiled=True).astype(s_wqkv.dtype),
        lax.all_gather(s_bqv.astype(jnp.bfloat16), "seq", axis=1, tiled=True).astype(s_bqv.dtype),
        lax.all_gather(s_wout.astype(jnp.bfloat16), "seq", axis=0, tiled=True).astype(s_wout.dtype),
        lax.all_gather(s_bout.astype(jnp.bfloat16), "seq", axis=0, tiled=True).astype(s_bout.dtype),
        lax.all_gather(s_wup.astype(jnp.bfloat16), "seq", axis=0, tiled=True).astype(s_wup.dtype),
        lax.all_gather(s_bup.astype(jnp.bfloat16), "seq", axis=0, tiled=True).astype(s_bup.dtype),
        lax.all_gather(s_wdown.astype(jnp.bfloat16), "seq", axis=0, tiled=True).astype(
            s_wdown.dtype
        ),
        lax.all_gather(s_bdown.astype(jnp.bfloat16), "seq", axis=0, tiled=True).astype(
            s_bdown.dtype
        ),
        lax.all_gather(s_bada.astype(jnp.bfloat16), "seq", axis=0, tiled=True).astype(s_bada.dtype),
    )
    t_wada, t_cond = (
        lax.psum(grad_w_ada, "seq").astype(jnp.float32),
        lax.psum(grad_cond_part.astype(jnp.bfloat16), "seq").astype(jnp.float32),
    )
    return (
        output,
        grad_tokens,
        t_cond,
        t_wada,
        t_bada,
        t_wqkv,
        t_bqv,
        t_wout,
        t_bout,
        t_wup,
        t_bup,
        t_wdown,
        t_bdown,
    )


def solution(mesh):
    in_specs = (
        P("fsdp", "seq", None),
        P("fsdp", None),
        P("fsdp", None),
        P("fsdp"),
        P("fsdp", None),
        P(None, "fsdp"),
        P("fsdp", None),
        P("fsdp"),
        P("fsdp", None),
        P("fsdp"),
        P("fsdp", None),
        P("fsdp"),
        P("fsdp", "seq", None),
    )
    out_specs = (
        P("fsdp", "seq", None),
        P("fsdp", "seq", None),
        P("fsdp", None),
        P("fsdp", None),
        P("fsdp"),
        P("fsdp", None),
        P(None, "fsdp"),
        P("fsdp", None),
        P("fsdp"),
        P("fsdp", None),
        P("fsdp"),
        P("fsdp", None),
        P("fsdp"),
    )
    return jax.shard_map(local, mesh=mesh, in_specs=in_specs, out_specs=out_specs, check_vma=False)
```

profile of v0, /device:TPU:0, one launch (start us, length us, event | category | flops | bytes accessed | tf_op | source)
XLA Modules:
  0.0 1821.9 jit_solution(10421692875912982630)
XLA Ops:
  13.2 22.8 %all-gather = bf16[8,144,2]{1,2,0:T(2,128)(2,1)S(1)} all-gather(bf16[1,144,2]{1,2,0:T(2,128)(2,1)S(1)} %bitcast.233), channel_id=1, replica_groups=mesh['fsdp'=8,'seq'=4] {'fsdp'}, dimensions={0}, use_global_device_ids=true | all-gather | bytes 5184 | tf_op jit(solution)/shard_map/all_gather | solution.py:126
  37.1 36.0 %all-reduce.20 = (bf16[6912]{0:T(1024)(128)(2,1)S(1)}, bf16[1152]{0:T(1024)(128)(2,1)}, bf16[1152]{0:T(1024)(128)(2,1)}, bf16[4608]{0:T(1024)(128)(2,1)}) all-reduce(bf16[6912]{0:T(1024)(128)(2,1)S(1)} %dynamic-update-slice, bf16[1152]{0:T(1024)(128)(2,1)S(1)} %dynamic-update-slice.1, ...), channel_id=1, replica_groups=mesh['fsdp'=8,'seq'=4] {'fsdp'}, use_global_device_ids=true, to_apply=%add | all-reduce | flops 13824 | bytes 55296
  73.7 156.8 %all-gather.13.cloned.1.call-done = bf16[1152,6912]{1,0:T(8,128)(2,1)} async-done(((bf16[144,6912]{1,0:T(8,128)(2,1)}), bf16[1152,6912]{1,0:T(8,128)(2,1)}) %all-gather.13.cloned.1.call-update) | async-done | bytes 15925264 | tf_op jit(solution)/shard_map/all_gather | solution.py:138
  230.4 7.7 convolution_reduce_fusion
  238.9 111.1 %all-gather.15.cloned.1.call-done = bf16[1152,3456]{1,0:T(8,128)(2,1)} async-done(((bf16[144,3456]{1,0:T(8,128)(2,1)}), bf16[1152,3456]{1,0:T(8,128)(2,1)}) %all-gather.15.cloned.1.call-update) | async-done | bytes 7962640 | tf_op jit(solution)/shard_map/all_gather | solution.py:125
  350.0 6.0 fusion.74
  360.4 6.2 reduce.42
  373.3 6.2 reduce.43
  387.6 6.2 reduce.44
  402.3 6.4 all-to-all-done.2
  411.9 8.5 multiply_reduce_fusion
  420.4 8.6 exponential_reduce_fusion
  429.0 9.6 convolution_convert_fusion.4
  442.9 6.5 reduce.45
  458.2 8.3 all-to-all-done.3
  480.4 77.7 %all-gather.19.cloned.1.call-done = bf16[1152,4608]{1,0:T(8,128)(2,1)} async-done(((bf16[144,4608]{1,0:T(8,128)(2,1)}), bf16[1152,4608]{1,0:T(8,128)(2,1)}) %all-gather.19.cloned.1.call-update) | async-done | bytes 10616848 | tf_op jit(solution)/shard_map/all_gather | solution.py:129
  558.1 6.2 convolution_add_fusion
  566.7 9.3 fusion.52
  577.3 133.2 %all-gather.21.cloned.1.call-done = bf16[4608,1152]{1,0:T(8,128)(2,1)} async-done(((bf16[576,1152]{1,0:T(8,128)(2,1)}), bf16[4608,1152]{1,0:T(8,128)(2,1)}) %all-gather.21.cloned.1.call-update) | async-done | bytes 10616848 | tf_op jit(solution)/shard_map/all_gather | solution.py:131
  710.4 8.9 fusion.85
  719.4 9.7 fusion.34
  729.9 10.6 fusion.18
  747.2 8.1 reduce.46
  757.4 13.9 all_to_all.129
  780.1 9.7 convolution_convert_fusion.1
  794.3 7.4 reduce.47
  811.2 11.1 multiply_convert_fusion.1
  830.5 7.4 reduce.48
  845.6 5.4 convolution_convert_fusion.3
  853.9 6.5 reduce.49
  900.7 7.3 fusion.29
  914.5 6.6 multiply_convert_fusion
  926.2 9.3 fusion.39
  935.6 8.1 fusion.43
  943.7 577.3 %fusion.80 = (f32[48,3456]{1,0:T(8,128)S(1)}, f32[48,1152]{1,0:T(8,128)S(1)}, f32[40,4608]{1,0:T(8,128)S(1)}) fusion(f32[1152,3456]{1,0:T(8,128)} %fusion.43, f32[1152,1152]{1,0:T(8,128)} %fusion.57, f32[1152,4608]{1,0:T(8,128)} %fusion.39), kind=kCustom, calls=%all-reduce-scatter.3 | all-reduce-scatter fusion | flops 12976130 | bytes 44089344
  1523.8 35.3 %collective-permute-start.17 = (bf16[40,4608]{1,0:T(8,128)(2,1)}, bf16[40,4608]{1,0:T(8,128)(2,1)}, u32[]{:S(2)}, u32[]{:S(2)}) collective-permute-start(bf16[40,4608]{1,0:T(8,128)(2,1)} %convert.54), channel_id=1, source_target_pairs={{0,2},{1,3},{2,4},{3,5},{4,6},{5,7},{6,8},{7,9},{8,10},{9,11},{10,... | collective-permute-start | bytes 1105928
  1563.7 9.3 collective-permute-done.19
  1573.0 16.8 concatenate.12
  1595.8 6.9 collective-permute-start.14
  1604.9 5.7 collective-permute-start.12
  1623.2 9.8 fusion.11
  1633.1 39.2 %all-reduce.19 = (bf16[6912]{0:T(1024)(128)(2,1)S(1)}, bf16[2,1152]{1,0:T(2,128)(2,1)S(1)}, bf16[1152]{0:T(1024)(128)(2,1)S(1)}, bf16[4608]{0:T(1024)(128)(2,1)S(1)}, bf16[1152]{0:T(1024)(128)(2,1)S(1)}) all-reduce(bf16[6912]{0:T(1024)(128)(2,1)S(1)} %copy-done.22, ...), channel_id=3, replica_groups=mesh['fsdp'=8,'seq'=4] {'fsdp','seq'}, use_global_device_ids=true, to_apply=%region_20.21.clone | all-reduce | flops 16128 | bytes 82944
  1686.7 5.0 all-gather.2
  1697.8 7.6 all-reduce.21
  1714.9 5.3 concatenate.11
  1729.7 27.9 %all-gather.3 = bf16[4,36,1152]{2,1,0:T(8,128)(2,1)S(1)} all-gather(bf16[1,36,1152]{2,1,0:T(8,128)(2,1)S(1)} %fusion.60), channel_id=1, replica_groups=mesh['fsdp'=8,'seq'=4] {'seq'}, dimensions={0}, use_global_device_ids=true | all-gather | bytes 414720 | tf_op jit(solution)/shard_map/all_gather | solution.py:260
  1758.6 33.7 %concatenate.10 = bf16[420,3456]{1,0:T(8,128)(2,1)} concatenate(bf16[36,3456]{1,0:T(8,128)(2,1)} %collective-permute-done.7, bf16[48,3456]{1,0:T(8,128)(2,1)S(1)} %collective-permute-done.6, bf16[48,3456]{1,0:T(8,128)(2,1)} %copy-done.18, bf16[48,3456]{1,0:T(8,128)(2,1)} %collective-permute-done.4, bf16[48,3456]{1,0:T(8,128)(2,1)} %collective-permute-done.3, ...), dimensions={0} | concatenate | bytes 6137856
  1793.4 10.4 all-gather.1
  (339 shorter events, 248.7 us)
Async XLA Ops:
  7.2 223.3 %all-gather.13.cloned.1.call-start = ((), (), s32[]{:S(2)}) async-start(), calls=%async_computation.10 | async-start | bytes 17915904 | tf_op jit(solution)/shard_map/all_gather | solution.py:138
  7.9 28.2 %copy-start.57 = (bf16[144]{0:T(256)(128)(2,1)S(1)}, bf16[144]{0:T(256)(128)(2,1)}, u32[]{:S(2)}) copy-start(bf16[144]{0:T(256)(128)(2,1)} %param.20) | copy-start | bytes 868
  7.9 28.4 %copy-start.58 = (bf16[144]{0:T(256)(128)(2,1)S(1)}, bf16[144]{0:T(256)(128)(2,1)}, u32[]{:S(2)}) copy-start(bf16[144]{0:T(256)(128)(2,1)} %param.24) | copy-start | bytes 868
  8.0 28.7 %copy-start.54 = (bf16[864]{0:T(1024)(128)(2,1)S(1)}, bf16[864]{0:T(1024)(128)(2,1)}, u32[]{:S(2)}) copy-start(bf16[864]{0:T(1024)(128)(2,1)} %param.16) | copy-start | bytes 5188
  8.0 28.9 %copy-start.55 = (bf16[576]{0:T(1024)(128)(2,1)S(1)}, bf16[576]{0:T(1024)(128)(2,1)}, u32[]{:S(2)}) copy-start(bf16[576]{0:T(1024)(128)(2,1)} %param.22) | copy-start | bytes 3460
  8.0 65.2 %copy-start.1 = (bf16[1,256,1152]{2,1,0:T(8,128)(2,1)S(1)}, bf16[1,256,1152]{2,1,0:T(8,128)(2,1)}, u32[]{:S(2)}) copy-start(bf16[1,256,1152]{2,1,0:T(8,128)(2,1)} %param.13) | copy-start | bytes 1769476
  8.0 342.0 %all-gather.15.cloned.1.call-start = ((), (), s32[]{:S(2)}) async-start(), calls=%async_computation.11 | async-start | bytes 8957952 | tf_op jit(solution)/shard_map/all_gather | solution.py:125
  8.7 466.4 %all-gather.17.cloned.1.call-start = ((), (), s32[]{:S(2)}) async-start(), calls=%async_computation.12 | async-start | bytes 2985984 | tf_op jit(solution)/shard_map/all_gather | solution.py:127
  9.5 221.0 %copy-start.28 = (f32[1,1152]{1,0:T(1,128)S(1)}, f32[1,1152]{1,0:T(1,128)}, u32[]{:S(2)}) copy-start(f32[1,1152]{1,0:T(1,128)} %param.14) | copy-start | bytes 13828
  9.5 548.6 %all-gather.19.cloned.1.call-start = ((), (), s32[]{:S(2)}) async-start(), calls=%async_computation.13 | async-start | bytes 11943936 | tf_op jit(solution)/shard_map/all_gather | solution.py:129
  10.1 700.4 %all-gather.21.cloned.1.call-start = ((), (), s32[]{:S(2)}) async-start(), calls=%async_computation.14 | async-start | bytes 11943936 | tf_op jit(solution)/shard_map/all_gather | solution.py:131
  73.3 276.6 %copy-start.36 = (f32[256]{0:T(256)}, f32[256]{0:T(256)S(1)}, u32[]{:S(2)}) copy-start(f32[256]{0:T(256)S(1)} %broadcast_multiply_fusion.5) | copy-start | bytes 3076
  73.6 276.3 %copy-start.43 = (f32[256]{0:T(256)}, f32[256]{0:T(256)S(1)}, u32[]{:S(2)}) copy-start(f32[256]{0:T(256)S(1)} %add_rsqrt_fusion.1) | copy-start | bytes 3076
  238.9 117.1 %copy-start.25 = (f32[1152]{0:T(1024)}, f32[1152]{0:T(1024)S(1)}, u32[]{:S(2)}) copy-start(f32[1152]{0:T(1024)S(1)} %get-tuple-element.76) | copy-start | bytes 13828
  367.5 13.1 all-to-all-start
  380.6 14.1 all-to-all-start.1
  394.7 13.9 all-to-all-start.2
  400.7 28.3 %copy-start.10 = (bf16[1024,4,72]{0,2,1:T(8,128)(2,1)}, bf16[1024,4,72]{0,2,1:T(8,128)(2,1)S(1)}, u32[]{:S(2)}) copy-start(bf16[1024,4,72]{0,2,1:T(8,128)(2,1)S(1)} %reshape.384) | copy-start | bytes 1769476
  452.8 13.7 all-to-all-start.3
  457.0 1161.4 %reduce-scatter.12.cloned.1.call-start = ((), (), s32[]{:S(2)}) async-start(), calls=%async_computation.17 | async-start | bytes 21897216 | tf_op jit(solution)/shard_map/reduce_scatter | solution.py:253
  805.2 36.1 %all-to-all-start.7 = ((bf16[4,2,36864]{2,1,0:T(2,128)(2,1)}), bf16[4,2,36864]{2,1,0:T(2,128)(2,1)}, u32[]{:S(2)}, u32[]{:S(2)}) async-start(bf16[4,2,36864]{2,1,0:T(2,128)(2,1)} %reshape.483), calls=%async_computation.7 | async-start | bytes 1179648 | tf_op jit(solution)/shard_map/all_to_all | solution.py:211
  841.3 21.1 %all-to-all-start.6 = ((bf16[4,2,36864]{2,1,0:T(2,128)(2,1)}), bf16[4,2,36864]{2,1,0:T(2,128)(2,1)}, u32[]{:S(2)}, u32[]{:S(2)}) async-start(bf16[4,2,36864]{2,1,0:T(2,128)(2,1)} %reshape.485), calls=%async_computation.6 | async-start | bytes 1179648 | tf_op jit(solution)/shard_map/all_to_all | solution.py:210
  862.3 27.8 %all-to-all-start.5 = ((bf16[4,2,36864]{2,1,0:T(2,128)(2,1)}), bf16[4,2,36864]{2,1,0:T(2,128)(2,1)}, u32[]{:S(2)}, u32[]{:S(2)}) async-start(bf16[4,2,36864]{2,1,0:T(2,128)(2,1)} %reshape.487), calls=%async_computation.5 | async-start | bytes 1179648 | tf_op jit(solution)/shard_map/all_to_all | solution.py:209
  866.5 853.7 %reduce-scatter.10.cloned.1.call-start = ((), (), s32[]{:S(2)}) async-start(), calls=%async_computation.15 | async-start | bytes 17915904 | tf_op jit(solution)/shard_map/reduce_scatter | solution.py:238
  921.1 884.0 %all-gather.25.cloned.1.call-start = ((), (), s32[]{:S(2)}) async-start(), calls=%async_computation.19 | async-start | bytes 1843200 | tf_op jit(solution)/shard_map/all_gather | solution.py:262
  1521.8 51.2 %collective-permute-start.18 = (bf16[40,4608]{1,0:T(8,128)(2,1)}, bf16[40,4608]{1,0:T(8,128)(2,1)}, u32[]{:S(2)}, u32[]{:S(2)}) collective-permute-start(bf16[40,4608]{1,0:T(8,128)(2,1)} %convert.54), channel_id=1, source_target_pairs={{0,3},{1,4},{2,5},{3,6},{4,7},{5,8},{6,9},{7,10},{8,11},{9,12},{10... | collective-permute-start | bytes 1105928
  1523.8 49.2 %collective-permute-start.17 = (bf16[40,4608]{1,0:T(8,128)(2,1)}, bf16[40,4608]{1,0:T(8,128)(2,1)}, u32[]{:S(2)}, u32[]{:S(2)}) collective-permute-start(bf16[40,4608]{1,0:T(8,128)(2,1)} %convert.54), channel_id=1, source_target_pairs={{0,2},{1,3},{2,4},{3,5},{4,6},{5,7},{6,8},{7,9},{8,10},{9,11},{10,... | collective-permute-start | bytes 1105928
  1559.1 13.9 collective-permute-start.16
  1562.2 10.8 collective-permute-start.19
  1563.6 28.1 %copy-start.59 = (u32[32]{0:T(128)S(1)}, u32[32]{0:T(128)}, u32[]{:S(2)}) copy-start(u32[32]{0:T(128)} %constant.92) | copy-start | bytes 388
  1591.7 216.2 %all-gather.23.cloned.1.call-start = ((), (), s32[]{:S(2)}) async-start(), calls=%async_computation.18 | async-start | bytes 1658880 | tf_op jit(solution)/shard_map/all_gather | solution.py:264
  1595.8 80.7 %collective-permute-start.14 = (bf16[48,1152]{1,0:T(8,128)(2,1)S(1)}, bf16[48,1152]{1,0:T(8,128)(2,1)S(1)}, u32[]{:S(2)}, u32[]{:S(2)}) collective-permute-start(bf16[48,1152]{1,0:T(8,128)(2,1)S(1)} %convert.56), channel_id=1, source_target_pairs={{0,7},{1,8},{2,9},{3,10},{4,11},{5,12},{6,13},{7,14},{8,15},{9,16}... | collective-permute-start | bytes 331784
  1602.7 78.8 %collective-permute-start.13 = (bf16[48,1152]{1,0:T(8,128)(2,1)S(1)}, bf16[48,1152]{1,0:T(8,128)(2,1)}, u32[]{:S(2)}, u32[]{:S(2)}) collective-permute-start(bf16[48,1152]{1,0:T(8,128)(2,1)S(1)} %convert.56), channel_id=1, source_target_pairs={{0,6},{1,7},{2,8},{3,9},{4,10},{5,11},{6,12},{7,13},{8,14},{9,15},... | collective-permute-start | bytes 331784
  1604.9 77.9 %collective-permute-start.12 = (bf16[48,1152]{1,0:T(8,128)(2,1)S(1)}, bf16[48,1152]{1,0:T(8,128)(2,1)}, u32[]{:S(2)}, u32[]{:S(2)}) collective-permute-start(bf16[48,1152]{1,0:T(8,128)(2,1)S(1)} %convert.56), channel_id=1, source_target_pairs={{0,5},{1,6},{2,7},{3,8},{4,9},{5,10},{6,11},{7,12},{8,13},{9,14},{... | collective-permute-start | bytes 331784
  1611.8 111.7 %collective-permute-start.6 = (bf16[48,3456]{1,0:T(8,128)(2,1)S(1)}, bf16[48,3456]{1,0:T(8,128)(2,1)S(1)}, u32[]{:S(2)}, u32[]{:S(2)}) collective-permute-start(bf16[48,3456]{1,0:T(8,128)(2,1)S(1)} %convert.55), channel_id=1, source_target_pairs={{0,7},{1,8},{2,9},{3,10},{4,11},{5,12},{6,13},{7,14},{8,15},{9,16}... | collective-permute-start | bytes 995336
  1613.1 59.2 %collective-permute-start.15 = (bf16[36,1152]{1,0:T(8,128)(2,1)}, bf16[36,1152]{1,0:T(8,128)(2,1)S(1)}, u32[]{:S(2)}, u32[]{:S(2)}) collective-permute-start(bf16[36,1152]{1,0:T(8,128)(2,1)} %slice.57), channel_id=1, source_target_pairs={{0,8},{1,9},{2,10},{3,11},{4,12},{5,13},{6,14},{7,15},{8,16},{9,17... | collective-permute-start | bytes 248840
  1620.2 190.6 %all-reduce.25.cloned.1.call-start = ((), (), s32[]{:S(2)}) async-start(), calls=%async_computation.16 | async-start | bytes 3981312 | tf_op jit(solution)/shard_map/psum | solution.py:273
  1672.3 55.3 %collective-permute-start.5 = (bf16[48,3456]{1,0:T(8,128)(2,1)S(1)}, bf16[48,3456]{1,0:T(8,128)(2,1)S(1)}, u32[]{:S(2)}, u32[]{:S(2)}) collective-permute-start(bf16[48,3456]{1,0:T(8,128)(2,1)S(1)} %convert.55), channel_id=1, source_target_pairs={{0,6},{1,7},{2,8},{3,9},{4,10},{5,11},{6,12},{7,13},{8,14},{9,15},... | collective-permute-start | bytes 995336
  1676.5 15.3 collective-permute-start.11
  1681.5 12.9 collective-permute-start.10
  1682.8 37.5 %collective-permute-start.7 = (bf16[36,3456]{1,0:T(8,128)(2,1)}, bf16[36,3456]{1,0:T(8,128)(2,1)}, u32[]{:S(2)}, u32[]{:S(2)}) collective-permute-start(bf16[36,3456]{1,0:T(8,128)(2,1)} %slice.56), channel_id=1, source_target_pairs={{0,8},{1,9},{2,10},{3,11},{4,12},{5,13},{6,14},{7,15},{8,16},{9,17... | collective-permute-start | bytes 746504
  1691.8 17.2 collective-permute-start.9
  1694.4 16.6 collective-permute-start.8
  1709.0 49.6 %collective-permute-start.4 = (bf16[48,3456]{1,0:T(8,128)(2,1)S(1)}, bf16[48,3456]{1,0:T(8,128)(2,1)}, u32[]{:S(2)}, u32[]{:S(2)}) collective-permute-start(bf16[48,3456]{1,0:T(8,128)(2,1)S(1)} %convert.55), channel_id=1, source_target_pairs={{0,5},{1,6},{2,7},{3,8},{4,9},{5,10},{6,11},{7,12},{8,13},{9,14},{... | collective-permute-start | bytes 995336
  1711.6 47.0 %collective-permute-start.3 = (bf16[48,3456]{1,0:T(8,128)(2,1)S(1)}, bf16[48,3456]{1,0:T(8,128)(2,1)}, u32[]{:S(2)}, u32[]{:S(2)}) collective-permute-start(bf16[48,3456]{1,0:T(8,128)(2,1)S(1)} %convert.55), channel_id=1, source_target_pairs={{0,4},{1,5},{2,6},{3,7},{4,8},{5,9},{6,10},{7,11},{8,12},{9,13},{1... | collective-permute-start | bytes 995336
  1720.3 38.3 %collective-permute-start.2 = (bf16[48,3456]{1,0:T(8,128)(2,1)S(1)}, bf16[48,3456]{1,0:T(8,128)(2,1)S(1)}, u32[]{:S(2)}, u32[]{:S(2)}) collective-permute-start(bf16[48,3456]{1,0:T(8,128)(2,1)S(1)} %convert.55), channel_id=1, source_target_pairs={{0,3},{1,4},{2,5},{3,6},{4,7},{5,8},{6,9},{7,10},{8,11},{9,12},{10... | collective-permute-start | bytes 995336
  1723.5 35.1 %collective-permute-start.1 = (bf16[48,3456]{1,0:T(8,128)(2,1)S(1)}, bf16[48,3456]{1,0:T(8,128)(2,1)}, u32[]{:S(2)}, u32[]{:S(2)}) collective-permute-start(bf16[48,3456]{1,0:T(8,128)(2,1)S(1)} %convert.55), channel_id=1, source_target_pairs={{0,2},{1,3},{2,4},{3,5},{4,6},{5,7},{6,8},{7,9},{8,10},{9,11},{10,... | collective-permute-start | bytes 995336
  1727.7 30.9 %collective-permute-start = (bf16[48,3456]{1,0:T(8,128)(2,1)S(1)}, bf16[48,3456]{1,0:T(8,128)(2,1)}, u32[]{:S(2)}, u32[]{:S(2)}) collective-permute-start(bf16[48,3456]{1,0:T(8,128)(2,1)S(1)} %convert.55), channel_id=1, source_target_pairs={{0,1},{1,2},{2,3},{3,4},{4,5},{5,6},{6,7},{7,8},{8,9},{9,10},{10,1... | collective-permute-start | bytes 995336
  (50 other events, 449.9 us)
Sparse Core Ops, SparseCore 0:
  10.2 220.2 all-gather.12
  232.6 117.2 all-gather.14
  352.1 53.1 all-gather.16
  407.4 150.6 all-gather.18
  560.1 150.2 all-gather.20
  716.7 223.6 reduce-scatter.11
  944.3 462.4 reduce-scatter.9
  1591.8 24.0 all-gather.24
  1620.4 22.4 all-gather.22
  1720.4 62.1 all-reduce.24
where the time goes:
time: 1840 us; the launch traced here: 1820 us
  blocking collectives  740 us (40%)
  waiting for transfers between devices  506 us (28%)
  local copies, waits for them, and re-layouts  184 us (10%)
  matrix products  152 us (8%)
  starting transfers between devices  124 us (7%)
  other arithmetic  95.9 us (5%)
  between operations  19.8 us (1%)
    unnamed x3, blocking collectives  653 us
    all_gather x1, waiting for transfers between devices, local(): full_ada = lax.all_gather(w_ada, 'fsdp', axis=0, tiled=True)  157 us
    all_gather x1, waiting for transfers between devices, local(): lax.all_gather(w_down, 'fsdp', axis=0, tiled=True)  133 us
    unnamed x177, local copies, waits for them, and re-layouts  114 us
    all_gather x1, waiting for transfers between devices, local(): lax.all_gather(w_qkv, 'fsdp', axis=0, tiled=True)  111 us
    unnamed x20, starting transfers between devices  95.3 us
    all_gather x1, waiting for transfers between devices, local(): lax.all_gather(w_up, 'fsdp', axis=0, tiled=True)  77.7 us
    unnamed x11, other arithmetic  55.2 us
  transfers between devices with their start and end apart: 37, of which 8 were waited for; matrix products, arithmetic and copies ran while one was open for 54% of the time, Pallas kernels for 0%

commit v1 on v0

--- a/solution.py
+++ b/solution.py
@@ -6,6 +6,11 @@
 HD = 72
 EPSILON = 1e-06
 GELU_C = 0.7978845608028654
+
+
+def gather_over(x, mesh_axis, dim):
+    sent = jnp.stack([x] * lax.axis_size(mesh_axis))
+    return jnp.concatenate(lax.all_to_all(sent, mesh_axis, 0, 0), axis=dim)
 
 
 def layer_norm(values):
@@ -122,7 +127,7 @@
     lat_dev, seq_loc, width = tokens.shape
     row_count = lat_dev * seq_loc
     full_qkv, full_bqv, full_out, full_bout, full_up, full_bup, full_down, full_bdown, full_bada = (
-        lax.all_gather(w_qkv, "fsdp", axis=0, tiled=True),
+        gather_over(w_qkv, "fsdp", 0),
         lax.all_gather(b_qv, "fsdp", axis=1, tiled=True),
         lax.all_gather(w_out, "fsdp", axis=0, tiled=True),
         lax.all_gather(b_out, "fsdp", axis=0, tiled=True),

time: 1840 us -> 1910 us (1.038)
  blocking collectives: 740 us -> 1130 us
  waiting for transfers between devices: 506 us -> 201 us
    all_gather x1, blocking collectives: 22.8 us -> 222 us  [local(): lax.all_gather(b_qv, 'fsdp', axis=1, tiled=True)]
    unnamed x3, blocking collectives: 653 us -> 843 us
    all_gather x1, waiting for transfers between devices: 157 us -> 0.02 us  [local(): full_ada = lax.all_gather(w_ada, 'fsdp', axis=0, tiled=True)]
    all_gather x1, waiting for transfers between devices: 111 us -> 0.01 us  [local(): lax.all_gather(w_qkv, 'fsdp', axis=0, tiled=True)]
    all_gather x1, waiting for transfers between devices: 77.7 us -> 46.7 us  [local(): lax.all_gather(w_up, 'fsdp', axis=0, tiled=True)]
    unnamed x20, starting transfers between devices: 95.3 us -> 73.4 us
  transfers between devices with their start and end apart: 37 -> 38, of which waited for: 8 -> 7; matrix products, arithmetic and copies ran while one was open for 54% -> 56% of each run, Pallas kernels for 0% -> 0%
where the time goes in v1:
time: 1910 us; the launch traced here: 1890 us
  blocking collectives  1130 us (59%)
  waiting for transfers between devices  201 us (11%)
  local copies, waits for them, and re-layouts  188 us (10%)
  matrix products  149 us (8%)
  starting transfers between devices  110 us (6%)
  other arithmetic  96.5 us (5%)
  between operations  19.8 us (1%)
    unnamed x3, blocking collectives  843 us
    all_gather x1, blocking collectives, local(): lax.all_gather(b_qv, 'fsdp', axis=1, tiled=True)  222 us
    all_gather x1, waiting for transfers between devices, local(): lax.all_gather(w_down, 'fsdp', axis=0, tiled=True)  133 us
    unnamed x177, local copies, waits for them, and re-layouts  113 us
    unnamed x20, starting transfers between devices  73.4 us
    unnamed x11, other arithmetic  55.8 us
    all_gather x1, waiting for transfers between devices, local(): lax.all_gather(w_up, 'fsdp', axis=0, tiled=True)  46.7 us
  transfers between devices with their start and end apart: 38, of which 7 were waited for; matrix products, arithmetic and copies ran while one was open for 56% of the time, Pallas kernels for 0%

profile of v1, /device:TPU:0, one launch (start us, length us, event | category | flops | bytes accessed | tf_op | source)
XLA Modules:
  0.0 1893.9 jit_solution(16945096521603027842)
XLA Ops:
  13.8 7.5 all-to-all-start
  24.4 221.6 %all-gather = bf16[8,144,2]{1,2,0:T(2,128)(2,1)S(1)} all-gather(bf16[1,144,2]{1,2,0:T(2,128)(2,1)S(1)} %bitcast.234), channel_id=1, replica_groups=mesh['fsdp'=8,'seq'=4] {'fsdp'}, dimensions={0}, use_global_device_ids=true | all-gather | bytes 5184 | tf_op jit(solution)/shard_map/all_gather | solution.py:131
  247.1 164.3 %all-reduce.20 = (bf16[6912]{0:T(1024)(128)(2,1)S(1)}, bf16[1152]{0:T(1024)(128)(2,1)}, bf16[1152]{0:T(1024)(128)(2,1)}, bf16[4608]{0:T(1024)(128)(2,1)}) all-reduce(bf16[6912]{0:T(1024)(128)(2,1)S(1)} %dynamic-update-slice, bf16[1152]{0:T(1024)(128)(2,1)S(1)} %dynamic-update-slice.1, ...), channel_id=1, replica_groups=mesh['fsdp'=8,'seq'=4] {'fsdp'}, use_global_device_ids=true, to_apply=%add | all-reduce | flops 13824 | bytes 55296
  412.0 7.7 convolution_reduce_fusion
  420.5 6.0 fusion.74
  431.0 6.2 reduce.42
  443.9 6.2 reduce.43
  458.5 6.2 reduce.44
  473.0 6.4 all-to-all-done.3
  482.7 8.2 multiply_reduce_fusion
  490.9 8.5 exponential_reduce_fusion
  499.5 9.5 convolution_convert_fusion.4
  513.2 6.6 reduce.45
  528.6 8.3 all-to-all-done.4
  550.6 46.7 %all-gather.17.cloned.1.call-done = bf16[1152,4608]{1,0:T(8,128)(2,1)} async-done(((bf16[144,4608]{1,0:T(8,128)(2,1)}), bf16[1152,4608]{1,0:T(8,128)(2,1)}) %all-gather.17.cloned.1.call-update) | async-done | bytes 10616848 | tf_op jit(solution)/shard_map/all_gather | solution.py:134
  597.3 6.2 convolution_add_fusion
  605.9 9.3 fusion.52
  616.5 133.2 %all-gather.19.cloned.1.call-done = bf16[4608,1152]{1,0:T(8,128)(2,1)} async-done(((bf16[576,1152]{1,0:T(8,128)(2,1)}), bf16[4608,1152]{1,0:T(8,128)(2,1)}) %all-gather.19.cloned.1.call-update) | async-done | bytes 10616848 | tf_op jit(solution)/shard_map/all_gather | solution.py:136
  749.7 8.9 fusion.85
  758.6 8.9 fusion.34
  768.3 9.8 fusion.18
  784.6 8.1 reduce.46
  794.8 13.9 all_to_all.134
  817.3 9.6 convolution_convert_fusion.1
  831.4 7.4 reduce.47
  848.3 11.1 multiply_convert_fusion.1
  867.4 7.4 reduce.48
  882.6 5.7 convolution_convert_fusion.3
  891.2 6.7 reduce.49
  931.9 4.7 copy.141
  939.3 7.1 fusion.29
  952.8 6.6 multiply_convert_fusion
  964.3 9.2 fusion.39
  973.5 8.2 fusion.43
  981.7 639.3 %fusion.80 = (f32[48,3456]{1,0:T(8,128)S(1)}, f32[48,1152]{1,0:T(8,128)S(1)}, f32[40,4608]{1,0:T(8,128)S(1)}) fusion(f32[1152,3456]{1,0:T(8,128)} %fusion.43, f32[1152,1152]{1,0:T(8,128)} %fusion.57, f32[1152,4608]{1,0:T(8,128)} %fusion.39), kind=kCustom, calls=%all-reduce-scatter.3 | all-reduce-scatter fusion | flops 12976130 | bytes 44089344
  1632.5 16.8 concatenate.12
  1655.2 12.8 collective-permute-start.14
  1668.0 10.9 collective-permute-start.13
  1678.9 5.0 collective-permute-start.12
  1695.6 9.8 fusion.11
  1705.4 39.0 %all-reduce.19 = (bf16[6912]{0:T(1024)(128)(2,1)S(1)}, bf16[2,1152]{1,0:T(2,128)(2,1)S(1)}, bf16[1152]{0:T(1024)(128)(2,1)S(1)}, bf16[4608]{0:T(1024)(128)(2,1)S(1)}, bf16[1152]{0:T(1024)(128)(2,1)S(1)}) all-reduce(bf16[6912]{0:T(1024)(128)(2,1)S(1)} %copy-done.22, ...), channel_id=3, replica_groups=mesh['fsdp'=8,'seq'=4] {'fsdp','seq'}, use_global_device_ids=true, to_apply=%region_20.21.clone | all-reduce | flops 16128 | bytes 82944
  1748.8 4.9 collective-permute-start.11
  1759.1 5.0 all-gather.2
  1770.0 7.6 all-reduce.21
  1786.7 5.3 concatenate.11
  1801.4 28.3 %all-gather.3 = bf16[4,36,1152]{2,1,0:T(8,128)(2,1)S(1)} all-gather(bf16[1,36,1152]{2,1,0:T(8,128)(2,1)S(1)} %fusion.60), channel_id=1, replica_groups=mesh['fsdp'=8,'seq'=4] {'seq'}, dimensions={0}, use_global_device_ids=true | all-gather | bytes 414720 | tf_op jit(solution)/shard_map/all_gather | solution.py:265
  1830.6 33.7 %concatenate.10 = bf16[420,3456]{1,0:T(8,128)(2,1)} concatenate(bf16[36,3456]{1,0:T(8,128)(2,1)} %collective-permute-done.7, bf16[48,3456]{1,0:T(8,128)(2,1)S(1)} %collective-permute-done.6, bf16[48,3456]{1,0:T(8,128)(2,1)} %copy-done.18, bf16[48,3456]{1,0:T(8,128)(2,1)} %collective-permute-done.4, bf16[48,3456]{1,0:T(8,128)(2,1)} %collective-permute-done.3, ...), dimensions={0} | concatenate | bytes 6137856
  1865.4 10.3 all-gather.1
  (342 shorter events, 243.5 us)
Async XLA Ops:
  7.2 404.8 %all-gather.13.cloned.1.call-start = ((), (), s32[]{:S(2)}) async-start(), calls=%async_computation.11 | async-start | bytes 17915904 | tf_op jit(solution)/shard_map/all_gather | solution.py:143
  7.9 537.4 %all-gather.15.cloned.1.call-start = ((), (), s32[]{:S(2)}) async-start(), calls=%async_computation.12 | async-start | bytes 2985984 | tf_op jit(solution)/shard_map/all_gather | solution.py:132
  8.7 588.6 %all-gather.17.cloned.1.call-start = ((), (), s32[]{:S(2)}) async-start(), calls=%async_computation.13 | async-start | bytes 11943936 | tf_op jit(solution)/shard_map/all_gather | solution.py:134
  9.4 740.2 %all-gather.19.cloned.1.call-start = ((), (), s32[]{:S(2)}) async-start(), calls=%async_computation.14 | async-start | bytes 11943936 | tf_op jit(solution)/shard_map/all_gather | solution.py:136
  13.7 232.4 %copy-start.57 = (bf16[144]{0:T(256)(128)(2,1)S(1)}, bf16[144]{0:T(256)(128)(2,1)}, u32[]{:S(2)}) copy-start(bf16[144]{0:T(256)(128)(2,1)} %param.20) | copy-start | bytes 868
  13.7 232.7 %copy-start.58 = (bf16[144]{0:T(256)(128)(2,1)S(1)}, bf16[144]{0:T(256)(128)(2,1)}, u32[]{:S(2)}) copy-start(bf16[144]{0:T(256)(128)(2,1)} %param.24) | copy-start | bytes 868
  13.7 232.9 %copy-start.54 = (bf16[864]{0:T(1024)(128)(2,1)S(1)}, bf16[864]{0:T(1024)(128)(2,1)}, u32[]{:S(2)}) copy-start(bf16[864]{0:T(1024)(128)(2,1)} %param.16) | copy-start | bytes 5188
  13.7 233.1 %copy-start.55 = (bf16[576]{0:T(1024)(128)(2,1)S(1)}, bf16[576]{0:T(1024)(128)(2,1)}, u32[]{:S(2)}) copy-start(bf16[576]{0:T(1024)(128)(2,1)} %param.22) | copy-start | bytes 3460
  13.7 397.7 %copy-start.1 = (bf16[1,256,1152]{2,1,0:T(8,128)(2,1)S(1)}, bf16[1,256,1152]{2,1,0:T(8,128)(2,1)}, u32[]{:S(2)}) copy-start(bf16[1,256,1152]{2,1,0:T(8,128)(2,1)} %param.13) | copy-start | bytes 1769476
  13.8 398.3 %copy-start.28 = (f32[1,1152]{1,0:T(1,128)S(1)}, f32[1,1152]{1,0:T(1,128)}, u32[]{:S(2)}) copy-start(f32[1,1152]{1,0:T(1,128)} %param.14) | copy-start | bytes 13828
  13.8 406.7 %all-to-all-start = ((bf16[8,144,3456]{2,1,0:T(8,128)(2,1)}), bf16[8,144,3456]{2,1,0:T(8,128)(2,1)}, u32[]{:S(2)}, u32[]{:S(2)}) async-start(bf16[8,144,3456]{2,1,0:T(8,128)(2,1)} %stack.41), calls=%async_computation | async-start | bytes 15925248 | tf_op jit(solution)/shard_map/all_to_all | solution.py:13
  21.2 918.0 %all-gather.21.cloned.1.call-start = ((), (), s32[]{:S(2)}) async-start(), calls=%async_computation.15 | async-start | bytes 8957952 | tf_op jit(solution)/shard_map/all_gather | solution.py:188
  438.1 13.1 all-to-all-start.1
  451.3 14.4 all-to-all-start.2
  465.7 13.7 all-to-all-start.3
  523.2 13.7 all-to-all-start.4
  527.4 1163.3 %reduce-scatter.12.cloned.1.call-start = ((), (), s32[]{:S(2)}) async-start(), calls=%async_computation.18 | async-start | bytes 21897216 | tf_op jit(solution)/shard_map/reduce_scatter | solution.py:258
  842.2 36.0 %all-to-all-start.8 = ((bf16[4,2,36864]{2,1,0:T(2,128)(2,1)}), bf16[4,2,36864]{2,1,0:T(2,128)(2,1)}, u32[]{:S(2)}, u32[]{:S(2)}) async-start(bf16[4,2,36864]{2,1,0:T(2,128)(2,1)} %reshape.489), calls=%async_computation.8 | async-start | bytes 1179648 | tf_op jit(solution)/shard_map/all_to_all | solution.py:216
  878.2 21.7 %all-to-all-start.7 = ((bf16[4,2,36864]{2,1,0:T(2,128)(2,1)}), bf16[4,2,36864]{2,1,0:T(2,128)(2,1)}, u32[]{:S(2)}, u32[]{:S(2)}) async-start(bf16[4,2,36864]{2,1,0:T(2,128)(2,1)} %reshape.491), calls=%async_computation.7 | async-start | bytes 1179648 | tf_op jit(solution)/shard_map/all_to_all | solution.py:215
  899.9 28.0 %all-to-all-start.6 = ((bf16[4,2,36864]{2,1,0:T(2,128)(2,1)}), bf16[4,2,36864]{2,1,0:T(2,128)(2,1)}, u32[]{:S(2)}, u32[]{:S(2)}) async-start(bf16[4,2,36864]{2,1,0:T(2,128)(2,1)} %reshape.493), calls=%async_computation.6 | async-start | bytes 1179648 | tf_op jit(solution)/shard_map/all_to_all | solution.py:214
  904.1 887.9 %reduce-scatter.10.cloned.1.call-start = ((), (), s32[]{:S(2)}) async-start(), calls=%async_computation.16 | async-start | bytes 17915904 | tf_op jit(solution)/shard_map/reduce_scatter | solution.py:243
  959.4 917.6 %all-gather.25.cloned.1.call-start = ((), (), s32[]{:S(2)}) async-start(), calls=%async_computation.20 | async-start | bytes 1843200 | tf_op jit(solution)/shard_map/all_gather | solution.py:267
  1621.8 29.4 %copy-start.59 = (u32[32]{0:T(128)S(1)}, u32[32]{0:T(128)}, u32[]{:S(2)}) copy-start(u32[32]{0:T(128)} %constant.92) | copy-start | bytes 388
  1621.8 9.2 collective-permute-start.18
  1623.9 8.5 collective-permute-start.17
  1626.0 6.5 collective-permute-start.16
  1628.0 2.9 collective-permute-start.19
  1649.3 34.6 %copy-start.19 = (bf16[1,6,1152]{2,1,0:T(8,128)(2,1)S(1)}, bf16[1,6,1152]{2,1,0:T(8,128)(2,1)}, u32[]{:S(2)}) copy-start(bf16[1,6,1152]{2,1,0:T(8,128)(2,1)} %stack.48) | copy-start | bytes 41476
  1651.1 228.7 %all-gather.23.cloned.1.call-start = ((), (), s32[]{:S(2)}) async-start(), calls=%async_computation.19 | async-start | bytes 1658880 | tf_op jit(solution)/shard_map/all_gather | solution.py:269
  1654.5 38.1 %copy-start.38 = (f32[256]{0:T(256)S(1)}, f32[256]{0:T(256)}, u32[]{:S(2)}) copy-start(f32[256]{0:T(256)} %copy-done.36) | copy-start | bytes 3076
  1654.5 38.2 %copy-start.45 = (f32[256]{0:T(256)S(1)}, f32[256]{0:T(256)}, u32[]{:S(2)}) copy-start(f32[256]{0:T(256)} %copy-done.43) | copy-start | bytes 3076
  1655.2 93.6 %collective-permute-start.14 = (bf16[48,1152]{1,0:T(8,128)(2,1)S(1)}, bf16[48,1152]{1,0:T(8,128)(2,1)S(1)}, u32[]{:S(2)}, u32[]{:S(2)}) collective-permute-start(bf16[48,1152]{1,0:T(8,128)(2,1)S(1)} %convert.56), channel_id=1, source_target_pairs={{0,7},{1,8},{2,9},{3,10},{4,11},{5,12},{6,13},{7,14},{8,15},{9,16}... | collective-permute-start | bytes 331784
  1668.0 85.8 %collective-permute-start.13 = (bf16[48,1152]{1,0:T(8,128)(2,1)S(1)}, bf16[48,1152]{1,0:T(8,128)(2,1)}, u32[]{:S(2)}, u32[]{:S(2)}) collective-permute-start(bf16[48,1152]{1,0:T(8,128)(2,1)S(1)} %convert.56), channel_id=1, source_target_pairs={{0,6},{1,7},{2,8},{3,9},{4,10},{5,11},{6,12},{7,13},{8,14},{9,15},... | collective-permute-start | bytes 331784
  1678.9 76.2 %collective-permute-start.12 = (bf16[48,1152]{1,0:T(8,128)(2,1)S(1)}, bf16[48,1152]{1,0:T(8,128)(2,1)}, u32[]{:S(2)}, u32[]{:S(2)}) collective-permute-start(bf16[48,1152]{1,0:T(8,128)(2,1)S(1)} %convert.56), channel_id=1, source_target_pairs={{0,5},{1,6},{2,7},{3,8},{4,9},{5,10},{6,11},{7,12},{8,13},{9,14},{... | collective-permute-start | bytes 331784
  1685.1 110.5 %collective-permute-start.6 = (bf16[48,3456]{1,0:T(8,128)(2,1)S(1)}, bf16[48,3456]{1,0:T(8,128)(2,1)S(1)}, u32[]{:S(2)}, u32[]{:S(2)}) collective-permute-start(bf16[48,3456]{1,0:T(8,128)(2,1)S(1)} %convert.55), channel_id=1, source_target_pairs={{0,7},{1,8},{2,9},{3,10},{4,11},{5,12},{6,13},{7,14},{8,15},{9,16}... | collective-permute-start | bytes 995336
  1688.0 56.4 %collective-permute-start.15 = (bf16[36,1152]{1,0:T(8,128)(2,1)}, bf16[36,1152]{1,0:T(8,128)(2,1)S(1)}, u32[]{:S(2)}, u32[]{:S(2)}) collective-permute-start(bf16[36,1152]{1,0:T(8,128)(2,1)} %slice.57), channel_id=1, source_target_pairs={{0,8},{1,9},{2,10},{3,11},{4,12},{5,13},{6,14},{7,15},{8,16},{9,17... | collective-permute-start | bytes 248840
  1692.6 190.2 %all-reduce.25.cloned.1.call-start = ((), (), s32[]{:S(2)}) async-start(), calls=%async_computation.17 | async-start | bytes 3981312 | tf_op jit(solution)/shard_map/psum | solution.py:278
  1744.5 54.9 %collective-permute-start.5 = (bf16[48,3456]{1,0:T(8,128)(2,1)S(1)}, bf16[48,3456]{1,0:T(8,128)(2,1)S(1)}, u32[]{:S(2)}, u32[]{:S(2)}) collective-permute-start(bf16[48,3456]{1,0:T(8,128)(2,1)S(1)} %convert.55), channel_id=1, source_target_pairs={{0,6},{1,7},{2,8},{3,9},{4,10},{5,11},{6,12},{7,13},{8,14},{9,15},... | collective-permute-start | bytes 995336
  1748.8 15.3 collective-permute-start.11
  1753.8 12.8 collective-permute-start.10
  1755.1 36.9 %collective-permute-start.7 = (bf16[36,3456]{1,0:T(8,128)(2,1)}, bf16[36,3456]{1,0:T(8,128)(2,1)}, u32[]{:S(2)}, u32[]{:S(2)}) collective-permute-start(bf16[36,3456]{1,0:T(8,128)(2,1)} %slice.56), channel_id=1, source_target_pairs={{0,8},{1,9},{2,10},{3,11},{4,12},{5,13},{6,14},{7,15},{8,16},{9,17... | collective-permute-start | bytes 746504
  1764.1 17.1 collective-permute-start.9
  1766.6 16.6 collective-permute-start.8
  1781.2 49.4 %collective-permute-start.4 = (bf16[48,3456]{1,0:T(8,128)(2,1)S(1)}, bf16[48,3456]{1,0:T(8,128)(2,1)}, u32[]{:S(2)}, u32[]{:S(2)}) collective-permute-start(bf16[48,3456]{1,0:T(8,128)(2,1)S(1)} %convert.55), channel_id=1, source_target_pairs={{0,5},{1,6},{2,7},{3,8},{4,9},{5,10},{6,11},{7,12},{8,13},{9,14},{... | collective-permute-start | bytes 995336
  1783.9 46.7 %collective-permute-start.3 = (bf16[48,3456]{1,0:T(8,128)(2,1)S(1)}, bf16[48,3456]{1,0:T(8,128)(2,1)}, u32[]{:S(2)}, u32[]{:S(2)}) collective-permute-start(bf16[48,3456]{1,0:T(8,128)(2,1)S(1)} %convert.55), channel_id=1, source_target_pairs={{0,4},{1,5},{2,6},{3,7},{4,8},{5,9},{6,10},{7,11},{8,12},{9,13},{1... | collective-permute-start | bytes 995336
  1792.0 38.6 %collective-permute-start.2 = (bf16[48,3456]{1,0:T(8,128)(2,1)S(1)}, bf16[48,3456]{1,0:T(8,128)(2,1)S(1)}, u32[]{:S(2)}, u32[]{:S(2)}) collective-permute-start(bf16[48,3456]{1,0:T(8,128)(2,1)S(1)} %convert.55), channel_id=1, source_target_pairs={{0,3},{1,4},{2,5},{3,6},{4,7},{5,8},{6,9},{7,10},{8,11},{9,12},{10... | collective-permute-start | bytes 995336
  1795.6 35.1 %collective-permute-start.1 = (bf16[48,3456]{1,0:T(8,128)(2,1)S(1)}, bf16[48,3456]{1,0:T(8,128)(2,1)}, u32[]{:S(2)}, u32[]{:S(2)}) collective-permute-start(bf16[48,3456]{1,0:T(8,128)(2,1)S(1)} %convert.55), channel_id=1, source_target_pairs={{0,2},{1,3},{2,4},{3,5},{4,6},{5,7},{6,8},{7,9},{8,10},{9,11},{10,... | collective-permute-start | bytes 995336
  1799.3 31.3 %collective-permute-start = (bf16[48,3456]{1,0:T(8,128)(2,1)S(1)}, bf16[48,3456]{1,0:T(8,128)(2,1)}, u32[]{:S(2)}, u32[]{:S(2)}) collective-permute-start(bf16[48,3456]{1,0:T(8,128)(2,1)S(1)} %convert.55), channel_id=1, source_target_pairs={{0,1},{1,2},{2,3},{3,4},{4,5},{5,6},{6,7},{7,8},{8,9},{9,10},{10,1... | collective-permute-start | bytes 995336
  (51 other events, 430.9 us)
Sparse Core Ops, SparseCore 0:
  10.2 378.0 all-gather.12
  390.4 53.8 all-gather.14
  446.5 150.7 all-gather.16
  599.3 150.2 all-gather.18
  751.7 117.2 all-gather.20
  875.3 299.9 reduce-scatter.11
  1179.2 422.8 reduce-scatter.9
  1651.3 36.3 all-gather.24
  1692.7 22.5 all-gather.22
  1792.1 62.4 all-reduce.24
